TPU v7x, 128 devices: a whole 4x4x4 slice. The times are simulated.
128 devices in a mesh: rows: 64 (over z, y, x), grp: 2 (over core).
Axes of the slice: x: 4, y: 4, z: 4, core: 2. Of those that a mesh axis runs over, the one named last changes fastest.
Arguments:
- earlier: bfloat16 [524288, 1024], P(('rows', 'grp')), may hold values from -6 to 6
- snapshots: bfloat16 [524288, 512], P(('rows', 'grp')), may hold values from -8 to 8
- later: bfloat16 [524288, 512], P(('rows', 'grp')), may hold values from -8 to 8
Outputs:
- basis: bfloat16 [524288, 512], P(('rows', 'grp'))
- factors: float32 [2, 256, 256], replicated
- shift_block: float32 [512, 512], replicated
All inputs are finite; a program needn't handle non-finite values.
Results may differ from a plain program's by a relative error of at most 0.0045.
The roundings to bfloat16 on the way count: a program that leaves them out, or rounds other values in their place, can miss the bound.
Values sent between devices are 32-bit elements; how exact they have to be, the bound alone decides.
A program may use at most 128 MiB of HBM per device.

v0:
```python
import functools
import itertools

import jax
import jax.numpy as jnp
from jax import lax
from jax.experimental import pallas as pl
from jax.experimental.pallas import tpu as pltpu
from jax.sharding import Mesh
from jax.sharding import PartitionSpec as P

PANEL = 256
BLOCK = 32
HALF = 128
F32 = jnp.float32
BF16 = jnp.bfloat16
MESH = pl.DeviceIdType.MESH
AXES = ("rows_0", "rows_1", "rows_2", "grp")


def thirds(value):
    top = value.astype(jnp.bfloat16)
    rest = value - top.astype(jnp.float32)
    middle = rest.astype(jnp.bfloat16)
    low = (rest - middle.astype(jnp.float32)).astype(jnp.bfloat16)
    return top, middle, low


def halves(value):
    top = value.astype(jnp.bfloat16)
    return top, (value - top.astype(jnp.float32)).astype(jnp.bfloat16)


def length_of(axis):
    return 2 if axis == "grp" or ":" in axis else 4


def size_of(stage):
    size = 1
    for axis in stage:
        size *= length_of(axis)
    return size


def offsets(stage):
    return [o for o in itertools.product(*[range(length_of(axis)) for axis in stage]) if any(o)]


def moved(axis, shift):
    name, _, pairing = axis.partition(":")
    at = lax.axis_index(name)
    if pairing == "a":
        return name, at + 1 - 2 * lax.rem(at, 2)
    if pairing == "b":
        return name, lax.rem(at + 3 + 2 * lax.rem(at, 2), 4)
    return name, lax.rem(at + shift, length_of(axis))


def part_of(axis, at):
    pairing = axis.partition(":")[2]
    if pairing == "a":
        return lax.rem((at + 1) // 2, 2)
    if pairing == "b":
        return at // 2
    return at


def peer_of(stage, offset):
    return dict(moved(axis, shift) for axis, shift in zip(stage, offset) if shift)


def place_in(stage, offset=None):
    place = 0
    for n, axis in enumerate(stage):
        at = moved(axis, offset[n])[1] if offset is not None and offset[n] else lax.axis_index(axis.partition(":")[0])
        place = place * length_of(axis) + part_of(axis, at)
    return place


def greet(stages):
    peers = []
    for stage in stages:
        for offset in offsets(stage):
            key = tuple(sorted((axis, shift) for axis, shift in zip(stage, offset) if shift))
            if key not in peers:
                peers.append(key)
    barrier = pltpu.get_barrier_semaphore()
    for key in peers:
        pl.semaphore_signal(
            barrier, inc=1, device_id=peer_of([a for a, _ in key], [n for _, n in key]), device_id_type=MESH
        )
    return lambda: pl.semaphore_wait(barrier, len(peers))


def levels_of(rows, stages):
    for stage in stages:
        rows //= size_of(stage)
        assert rows % 8 == 0
        yield stage, offsets(stage), rows


def stream_scratch(streams):
    shapes = []
    for _, rows, stages in streams:
        for stage, offs, length in levels_of(rows, stages):
            shapes += [pltpu.VMEM((len(offs), length, HALF), F32), pltpu.VMEM((length, HALF), F32)]
            shapes += [pltpu.SemaphoreType.DMA((len(offs),))] * 4
    return shapes


def copy_to(src, dst, send, recv, stage, offset):
    return pltpu.make_async_remote_copy(
        src_ref=src, dst_ref=dst, send_sem=send, recv_sem=recv, device_id=peer_of(stage, offset), device_id_type=MESH
    )


def stream(x_ref, o_ref, start, rows, stages, scratch, sent):
    levels = [level + tuple(next(scratch) for _ in range(6)) for level in levels_of(rows, stages)]
    where, src, base = start, x_ref, start
    for n, (stage, offs, length, slots, acc, send, recv, _, _) in enumerate(levels):
        copies = []
        for k, offset in enumerate(offs):
            at = pl.multiple_of(base + place_in(stage, offset) * length, 8)
            copies.append(copy_to(src.at[pl.ds(at, length), :], slots.at[k], send.at[k], recv.at[k], stage, offset))
            copies[-1].start()
        sent += copies
        yield
        own = place_in(stage) * length
        for copy in copies:
            copy.wait_recv()
        value = src[pl.ds(pl.multiple_of(base + own, 8), length), :]
        for k in range(len(offs)):
            value = value + slots[k]
        where = where + own
        if n + 1 < len(levels):
            acc[...] = value
        else:
            o_ref[pl.ds(pl.multiple_of(where, 8), length), :] = value
        src, base = acc, 0
    for stage, offs, length, _, _, _, _, send, recv in reversed(levels):
        piece = o_ref.at[pl.ds(pl.multiple_of(where, 8), length), :]
        copies = [copy_to(piece, piece, send.at[k], recv.at[k], stage, offset) for k, offset in enumerate(offs)]
        for copy in copies:
            copy.start()
        sent += copies
        yield
        for copy in copies:
            copy.wait_recv()
        where = where - place_in(stage) * length


def advance(streams):
    for one in streams:
        next(one, None)


G, X, Y, Z = "grp", "rows_2", "rows_1", "rows_0"
ORDERS = [((G,), (X,), (Y,), (Z,)), ((G,), (Y,), (Z,), (X,)), ((G,), (Z,), (X,), (Y,))]
PLANES = [((G,), (X,), (Y, Z)), ((G,), (Y,), (Z, X)), ((G,), (Z,), (X, Y))]
AT_ONCE = [((G,), (X, Y, Z))]


def colored(rows, orders, count):
    return [(n * rows // count, rows // count, orders[n % len(orders)]) for n in range(count)]


def factor(work, upper_ref, inverse_ref):
    lane = lax.broadcasted_iota(jnp.int32, (BLOCK, PANEL), 1)
    sub = lax.broadcasted_iota(jnp.int32, (BLOCK, HALF), 0)
    lane_half = lax.broadcasted_iota(jnp.int32, (BLOCK, HALF), 1)
    for k in range(PANEL // BLOCK):
        at = k * BLOCK
        rows = work[at : at + BLOCK, :]
        base = at // HALF * HALF
        off = at - base
        diag = rows[:, base : base + HALF]
        cols = [jnp.broadcast_to(diag[:, off + j : off + j + 1], (BLOCK, HALF)) for j in range(BLOCK)]
        eye = (lane_half == sub + off).astype(jnp.float32)
        wide = [rows[:, :HALF], rows[:, HALF:]]
        own = base // HALF
        inside = (lane_half >= off) & (lane_half < off + BLOCK)
        wide[own] = jnp.where(inside, eye, wide[own])
        scale = jnp.zeros((BLOCK, HALF), jnp.float32)
        for j in range(BLOCK):
            pivot = jnp.broadcast_to(cols[j][j : j + 1, :], (BLOCK, HALF))
            scale = jnp.where(sub == j, pivot, scale)
            if j == BLOCK - 1:
                break
            ratio = cols[j] * (1.0 / pivot)
            ratio = jnp.where(sub > j, ratio, 0.0)
            for m in range(j + 1, BLOCK):
                cols[m] = cols[m] - ratio * jnp.broadcast_to(cols[j][m : m + 1, :], (BLOCK, HALF))
            for h in range(2):
                wide[h] = wide[h] - ratio * jnp.broadcast_to(wide[h][j : j + 1, :], (BLOCK, HALF))
            diag = diag - ratio * jnp.broadcast_to(diag[j : j + 1, :], (BLOCK, HALF))
        scale = lax.rsqrt(scale)
        done = jnp.concatenate([wide[0] * scale, wide[1] * scale], axis=1)
        inverse_ref[at : at + BLOCK, :] = jnp.where(lane < at + BLOCK, done, 0.0)
        upper_ref[at : at + BLOCK, :] = jnp.where(lane >= at + BLOCK, done, 0.0)
        upper_ref[at : at + BLOCK, base : base + HALF] = jnp.where(
            inside & (lane_half - off >= sub), diag * scale, upper_ref[at : at + BLOCK, base : base + HALF]
        )
        if at + BLOCK < PANEL:
            a, b, c = thirds(done)
            right = jnp.concatenate([a, b, a, c, a, b], axis=0)
            left = jnp.concatenate([a, a, b, a, c, b], axis=0)
            prod = lax.dot_general(left.T[at + BLOCK :, :], right, (((1,), (0,)), ((), ())), preferred_element_type=jnp.float32)
            rest = work[at + BLOCK :, :]
            lanes = lax.broadcasted_iota(jnp.int32, rest.shape, 1)
            rest = jnp.where((lanes >= at) & (lanes < at + BLOCK), 0.0, rest)
            work[at + BLOCK :, :] = rest - prod
        yield


WIDTH = 1024
STEP = 1024
EARLY_ROWS = 9216
FIRST_ROWS = 1024
LAST_ROWS = 3072


def dot(left, right):
    return jnp.dot(left, right, preferred_element_type=F32)


def exact(left, right):
    return jnp.dot(left, right, precision=lax.Precision.HIGHEST, preferred_element_type=F32)


PAIRS = [(i, j) for j in range(4) for i in range(j + 1)]


def span(n, length=PANEL):
    return slice(n * length, (n + 1) * length)


def put_slabs(ref, at, value):
    rows = value.shape[0]
    for n in range(value.shape[1] // HALF):
        ref[at + n * rows : at + (n + 1) * rows, :] = value[:, span(n, HALF)]


def add_slabs(ref, at, value):
    rows = value.shape[0]
    for n in range(value.shape[1] // HALF):
        ref[at + n * rows : at + (n + 1) * rows, :] += value[:, span(n, HALF)]


def read_slabs(ref, at, rows, columns):
    return jnp.concatenate([ref[at + n * rows : at + (n + 1) * rows, :] for n in range(columns // HALF)], axis=1)


def add_gram(top, low, others, out_ref, mixed):
    top_t, low_t = top.T, low.T
    add_slabs(out_ref, 0, dot(top_t, top) + dot(low_t, low))
    mixed[...] += dot(top_t, low)
    if others is not None:
        add_slabs(out_ref, 512, dot(top_t, others) + dot(low_t, others))


def close_gram(out_ref, mixed):
    value = mixed[...]
    add_slabs(out_ref, 0, value + value.T)


EARLY_STREAMS = colored(EARLY_ROWS, ORDERS, 9)


def first_kernel(
    total, earlier_hbm, panels_hbm,
    top_hbm, low_hbm, flat_hbm, second_hbm, left_hbm, meet_hbm, out_hbm,
    second_ref, left_ref, meet_ref, out_ref, earlier, panels, turned, partial, sums, off, coeffs, near, mixed, top_all, low_all, flat_all, load, save, *scratch,
):
    ready = greet(ORDERS[0])
    scale = 1.0 / total
    chunks = earlier.shape[0] // 512
    loads = []
    for n in range(chunks):
        at = pl.ds(n * 512, 512)
        loads.append((
            pltpu.make_async_copy(earlier_hbm.at[at, :], earlier.at[at, :], load.at[0, n]),
            pltpu.make_async_copy(panels_hbm.at[at, :], panels.at[at, :], load.at[1, n]),
        ))
        for copy in loads[-1]:
            copy.start()
    for n in range(chunks):
        loads[n][0].wait()
        for i in range(4):
            turned[span(i), span(n, 512)] = earlier[span(n, 512), span(i)].T
    for n in range(chunks):
        loads[n][1].wait()

    @pl.loop(0, 4)
    def _(i):
        value = dot(turned[pl.ds(pl.multiple_of(i * PANEL, PANEL), PANEL), :], panels[...])
        for n in range(4):
            partial[pl.ds(pl.multiple_of(n * WIDTH + i * PANEL, PANEL), PANEL), :] = value[:, span(n, HALF)]

    scratch, sent = iter(scratch), []
    running = [stream(partial, sums, *one, scratch, sent) for one in EARLY_STREAMS]
    lead, rest = running[:4], running[4:]

    def gram_columns(j):
        for i in range(j + 1):
            put_slabs(partial, 4 * WIDTH + PAIRS.index((i, j)) * 512, dot(turned[span(i), :], earlier[:, span(j)]))

    ready()
    advance(lead)
    gram_columns(3)
    advance(lead)
    for j in range(3):
        gram_columns(j)
    advance(rest)
    for _ in range(7):
        advance(lead)
        advance(rest)

    for n in range(4):
        value = (sums[span(n, WIDTH), :] * scale).astype(BF16)
        coeffs[:WIDTH, span(n, HALF)] = value
        coeffs[WIDTH:, span(n, HALF)] = value

    @pl.loop(0, earlier.shape[0] // (2 * STEP))
    def _(n):
        for k in range(2):
            at = pl.ds(pl.multiple_of((2 * n + k) * STEP, STEP), STEP)
            flat = panels[at, :].astype(F32) - dot(earlier[at, :], coeffs[:WIDTH, :])
            top_all[at, :] = flat[:, :PANEL].astype(BF16)
            flat_all[at, :] = flat[:, PANEL:]

    saves = [pltpu.make_async_copy(flat_all, flat_hbm, save.at[0])]
    saves[0].start()
    advance(rest)

    for n, (i, j) in enumerate(PAIRS):
        block = read_slabs(sums, 4 * WIDTH + n * 512, PANEL, PANEL) * scale
        if i == j:
            rows = lax.broadcasted_iota(jnp.int32, block.shape, 0)
            columns = lax.broadcasted_iota(jnp.int32, block.shape, 1)
            block = block - (rows == columns).astype(F32)
        for k, value in enumerate(halves(block)):
            off[span(i), k * WIDTH + j * PANEL : k * WIDTH + (j + 1) * PANEL] = value
            if i != j:
                off[span(j), k * WIDTH + i * PANEL : k * WIDTH + (i + 1) * PANEL] = value.T
    beyond = dot(off[...], coeffs[...])
    for n in range(4):
        value = sums[span(n, WIDTH), :] * scale
        value = value - coeffs[:WIDTH, span(n, HALF)].astype(F32) - beyond[:, span(n, HALF)]
        if n < 2:
            near[:WIDTH, span(n, HALF)] = value.astype(BF16)
            near[WIDTH:, span(n, HALF)] = value.astype(BF16)
            left_ref[:, span(n, HALF)] = value - value.astype(BF16).astype(F32)
        else:
            second_ref[:, span(n - 2, HALF)] = value

    out_ref[...] = jnp.zeros_like(out_ref)
    mixed[...] = jnp.zeros_like(mixed)

    @pl.loop(0, earlier.shape[0] // (2 * STEP))
    def _(n):
        for k in range(2):
            at = pl.ds(pl.multiple_of((2 * n + k) * STEP, STEP), STEP)
            twice = top_all[at, :].astype(F32) - dot(earlier[at, :], near[:WIDTH, :])
            top, low = halves(twice)
            top_all[at, :] = top
            low_all[at, :] = low
            add_gram(top, low, panels[at, PANEL:], out_ref, mixed)

    saves += [pltpu.make_async_copy(top_all, top_hbm, save.at[1]), pltpu.make_async_copy(low_all, low_hbm, save.at[2])]
    saves[1].start()
    saves[2].start()
    close_gram(out_ref, mixed)
    saves.append(pltpu.make_async_copy(out_ref, out_hbm, save.at[3]))
    saves.append(pltpu.make_async_copy(second_ref, second_hbm, save.at[4]))
    for copy in saves[3:]:
        copy.start()
    left = left_ref[...] - dot(off[...], near[...])
    left_ref[...] = left
    left_t = left.T
    top, low = halves(left_t)
    meet_ref[...] = dot(top, coeffs[:WIDTH, PANEL:]) + dot(low, coeffs[:WIDTH, PANEL:])
    saves.append(pltpu.make_async_copy(left_ref, left_hbm, save.at[5]))
    saves.append(pltpu.make_async_copy(meet_ref, meet_hbm, save.at[6]))
    for copy in saves[5:]:
        copy.start()
    for copy in saves:
        copy.wait()
    for copy in sent:
        copy.wait_send()


def normalized(top, low, turned_top, turned_low):
    return (dot(top, turned_top) + (dot(top, turned_low) + dot(low, turned_top))).astype(BF16)


FIRST_STREAMS = [(0, FIRST_ROWS, ((G,), (X, Y), (Z,)))]
LAST_STREAMS = colored(LAST_ROWS, PLANES, 3)
SHIFT_AT = 512
AHEAD_AT = 1536


def second_kernel(
    total, part_hbm, left_hbm, second_hbm, meet_hbm, top_hbm, low_hbm, flat_hbm, earlier_hbm, later_hbm,
    basis_hbm, upper_hbm, newtop_hbm, newlow_hbm, last_hbm,
    part_ref, left_ref, second_ref, meet_ref, top_all, low_all, flat_all, earlier, later,
    basis, upper, sums, partial, last, work, inverse, turned_top, turned_low,
    fresh_b, near_e, near_q, mixed, load, save, *scratch,
):
    ready = greet([stage for _, _, stages in FIRST_STREAMS + LAST_STREAMS for stage in stages])
    scale = 1.0 / total
    loads = [
        pltpu.make_async_copy(src, dst, load.at[n])
        for n, (src, dst) in enumerate([
            (part_hbm, part_ref), (left_hbm, left_ref), (second_hbm, second_ref), (meet_hbm, meet_ref), (top_hbm, top_all),
            (low_hbm, low_all), (flat_hbm, flat_all), (earlier_hbm, earlier), (later_hbm, later),
        ])
    ]
    for copy in loads:
        copy.start()
    scratch, sent = iter(scratch), []
    running = [stream(part_ref, sums, *one, scratch, sent) for one in FIRST_STREAMS]
    ready()
    loads[0].wait()
    for _ in range(7):
        advance(running)
    for copy in loads[1:]:
        copy.wait()

    work[...] = read_slabs(sums, 0, PANEL, PANEL) * scale
    for _ in factor(work, upper, inverse):
        pass
    turn = inverse[...].T
    turned_top[...], turned_low[...] = halves(turn)
    fresh = exact(inverse[...], read_slabs(sums, 512, PANEL, PANEL) * scale)
    fresh_b[...] = fresh.astype(BF16)
    rounded = fresh.astype(BF16).astype(F32)
    near_q[...] = (fresh - rounded - exact(inverse[...], meet_ref[...])).astype(BF16)
    work[...] = exact(turn, rounded)

    @pl.loop(0, 4)
    def _(n):
        at = pl.ds(pl.multiple_of(n * PANEL, PANEL), PANEL)
        near_e[at, :] = (second_ref[at, :] - exact(left_ref[at, :], work[...])).astype(BF16)

    partial[...] = jnp.zeros_like(partial)
    mixed[...] = jnp.zeros_like(mixed)

    @pl.loop(0, earlier.shape[0] // STEP)
    def _(n):
        at = pl.ds(pl.multiple_of(n * STEP, STEP), STEP)
        newcols = normalized(top_all[at, :], low_all[at, :], turned_top[...], turned_low[...])
        basis[at, :] = newcols
        once = (flat_all[at, :] - dot(newcols, fresh_b[...])).astype(BF16)
        twice = once.astype(F32) - (dot(earlier[at, :], near_e[...]) + dot(newcols, near_q[...]))
        top, low = halves(twice)
        top_all[at, :] = top
        low_all[at, :] = low
        add_gram(top, low, None, partial, mixed)
        add_slabs(partial, SHIFT_AT, dot(newcols.T, later[at, :]))

    saves = [
        pltpu.make_async_copy(src, dst, save.at[n])
        for n, (src, dst) in enumerate([
            (basis, basis_hbm), (upper, upper_hbm), (top_all, newtop_hbm), (low_all, newlow_hbm), (last, last_hbm)
        ])
    ]
    for copy in saves[:4]:
        copy.start()
    close_gram(partial, mixed)
    running = [stream(partial, last, *one, scratch, sent) for one in LAST_STREAMS]
    lead, rest = running[:1], running[1:]
    advance(lead)

    @pl.loop(0, earlier.shape[0] // STEP)
    def _(n):
        at = pl.ds(pl.multiple_of(n * STEP, STEP), STEP)
        later_rows = later[at, :]
        add_slabs(partial, AHEAD_AT, dot(top_all[at, :].T, later_rows) + dot(low_all[at, :].T, later_rows))

    advance(lead)
    for _ in range(7):
        advance(rest)
        advance(lead)
    saves[4].start()
    for copy in saves:
        copy.wait()
    for copy in sent:
        copy.wait_send()


def third_kernel(
    total, sums_ref, first_upper_ref, first_ref, top_ref, low_ref, factors_ref, shift_ref, basis_ref,
    work, inverse, turned_top, turned_low,
):
    @pl.when(pl.program_id(0) == 0)
    def _():
        scale = 1.0 / total
        work[...] = read_slabs(sums_ref, 0, PANEL, PANEL) * scale
        factors_ref[0] = first_upper_ref[...]
        for _ in factor(work, factors_ref.at[1], inverse):
            pass
        turned_top[...], turned_low[...] = halves(inverse[...].T)
        shift_ref[:PANEL, :] = read_slabs(sums_ref, SHIFT_AT, PANEL, 512) * scale
        shift_ref[PANEL:, :] = exact(inverse[...], read_slabs(sums_ref, AHEAD_AT, PANEL, 512) * scale)

    basis_ref[:, :PANEL] = first_ref[...]
    basis_ref[:, PANEL:] = normalized(top_ref[...], low_ref[...], turned_top[...], turned_low[...])


def whole(*shape):
    return pl.BlockSpec(shape, lambda n: (0,) * len(shape))


def rows(columns):
    return pl.BlockSpec((2 * STEP, columns), lambda n: (n, 0))


def shape(*lengths, dtype=F32):
    return jax.ShapeDtypeStruct(lengths, dtype)


def body(earlier, snapshots, later):
    local = earlier.shape[0]
    total = local * lax.axis_size(AXES)
    square = pltpu.VMEM((PANEL, PANEL), F32)
    small = pltpu.VMEM((PANEL, PANEL), BF16)
    tall = pltpu.VMEM((WIDTH, PANEL), F32)
    outside = pl.BlockSpec(memory_space=pl.ANY)

    top, low, flat, second, left, meet, partial = pl.pallas_call(
        functools.partial(first_kernel, total),
        in_specs=[outside] * 2,
        out_specs=[outside] * 7,
        out_shape=[shape(local, PANEL, dtype=BF16), shape(local, PANEL, dtype=BF16), shape(local, PANEL),
                   shape(WIDTH, PANEL), shape(WIDTH, PANEL), shape(PANEL, PANEL), shape(FIRST_ROWS, HALF)],
        scratch_shapes=[tall, tall, square, pltpu.VMEM((FIRST_ROWS, HALF), F32),
                        pltpu.VMEM((local, WIDTH), BF16), pltpu.VMEM((local, 512), BF16), pltpu.VMEM((WIDTH, local), BF16),
                        pltpu.VMEM((EARLY_ROWS, HALF), F32), pltpu.VMEM((EARLY_ROWS, HALF), F32),
                        pltpu.VMEM((WIDTH, 2 * WIDTH), BF16), pltpu.VMEM((2 * WIDTH, 512), BF16),
                        pltpu.VMEM((2 * WIDTH, PANEL), BF16), square,
                        pltpu.VMEM((local, PANEL), BF16), pltpu.VMEM((local, PANEL), BF16), pltpu.VMEM((local, PANEL), F32),
                        pltpu.SemaphoreType.DMA((2, local // 512)), pltpu.SemaphoreType.DMA((7,))]
        + stream_scratch(EARLY_STREAMS),
        compiler_params=pltpu.CompilerParams(collective_id=1, has_side_effects=True, vmem_limit_bytes=62 * 2**20),
        name="first",
    )(earlier, snapshots)
    panel = pltpu.VMEM((local, PANEL), BF16)
    first, upper, top, low, last = pl.pallas_call(
        functools.partial(second_kernel, total),
        in_specs=[outside] * 9,
        out_specs=[outside] * 5,
        out_shape=[shape(local, PANEL, dtype=BF16), shape(PANEL, PANEL), shape(local, PANEL, dtype=BF16),
                   shape(local, PANEL, dtype=BF16), shape(LAST_ROWS, HALF)],
        scratch_shapes=[pltpu.VMEM((FIRST_ROWS, HALF), F32), tall, tall, square, panel, panel, pltpu.VMEM((local, PANEL), F32),
                        pltpu.VMEM((local, WIDTH), BF16), pltpu.VMEM((local, 512), BF16), panel, square,
                        pltpu.VMEM((FIRST_ROWS, HALF), F32), pltpu.VMEM((LAST_ROWS, HALF), F32), pltpu.VMEM((LAST_ROWS, HALF), F32),
                        square, square, small, small, small, pltpu.VMEM((WIDTH, PANEL), BF16), small, square,
                        pltpu.SemaphoreType.DMA((9,)), pltpu.SemaphoreType.DMA((5,))]
        + stream_scratch(FIRST_STREAMS + LAST_STREAMS),
        compiler_params=pltpu.CompilerParams(collective_id=2, has_side_effects=True, vmem_limit_bytes=60 * 2**20),
        name="second",
    )(partial, left, second, meet, top, low, flat, earlier, later)
    factors, shift_block, basis = pl.pallas_call(
        functools.partial(third_kernel, total),
        grid=(local // (2 * STEP),),
        in_specs=[whole(LAST_ROWS, HALF), whole(PANEL, PANEL), rows(PANEL), rows(PANEL), rows(PANEL)],
        out_specs=[whole(2, PANEL, PANEL), whole(512, 512), rows(512)],
        out_shape=[shape(2, PANEL, PANEL), shape(512, 512), shape(local, 512, dtype=BF16)],
        scratch_shapes=[square, square, small, small],
        compiler_params=pltpu.CompilerParams(dimension_semantics=("arbitrary",), vmem_limit_bytes=63 * 2**20),
        name="third",
    )(last, upper, first, top, low)
    return (basis, factors, shift_block)


def solution(mesh):
    torus = Mesh(mesh.devices.reshape(4, 4, 4, mesh.shape["grp"]), AXES)
    spec = P(AXES, None)
    return jax.shard_map(
        body, mesh=torus, in_specs=(spec, spec, spec), out_specs=(spec, P(), P()), check_vma=False
    )
```

profile of v0, /device:TPU:1, one launch (start us, length us, event | category | flops | bytes accessed | tf_op | source)
XLA Modules:
  0.0 174.4 jit_solution(17967841254331004701)
XLA Ops:
  0.6 75.7 %first.1 = (bf16[4096,256]{1,0:T(8,128)(2,1)}, bf16[4096,256]{1,0:T(8,128)(2,1)}, f32[4096,256]{1,0:T(8,128)}, f32[1024,256]{1,0:T(8,128)}, f32[1024,256]{1,0:T(...) custom-call(bf16[4096,1024]{1,0:T(8,128)(2,1)} %earlier_hbm.3, bf16[4096,512]{1,0:T(8,128)(2,1)} %panels_hbm.1), custom_call_target="tpu_custom_call" | custom-call | tf_op jit(solution)/shard_map/first/pallas_call | solution.py:530
  76.3 84.9 %second.1 = (bf16[4096,256]{1,0:T(8,128)(2,1)}, f32[256,256]{1,0:T(8,128)}, bf16[4096,256]{1,0:T(8,128)(2,1)}, bf16[4096,256]{1,0:T(8,128)(2,1)}, f32[3072,128]{1,0:T(8,128)}) custom-call(f32[1024,128]{1,0:T(8,128)} %get-tuple-element.18.part_hbm, f32[1024,256]{1,0:T(8,128)} %get-tuple-element.19.left_hbm, f32[1024,256]{1,0:T(8,128)} %get-tuple-element.20.second_hbm, ...), custom_call_target="tpu_custom_call" | custom-call | tf_op jit(solution)/shard_map/second/pallas_call | solution.py:548
  161.2 13.1 %third.1 = (f32[2,256,256]{2,1,0:T(8,128)}, f32[512,512]{1,0:T(8,128)}, bf16[4096,512]{1,0:T(8,128)(2,1)}) custom-call(f32[3072,128]{1,0:T(8,128)} %get-tuple-element.25.sums_ref, f32[256,256]{1,0:T(8,128)} %get-tuple-element.26.first_upper_ref, bf16[4096,256]{1,0:T(8,128)(2,1)} %get-tuple-element.27.first_ref, bf16[4096,256]{1,0:T(8,128)(2,1)} %get-tuple-element.28.top_ref, ...), custom_call_target="tpu_custom_call" | custom-call | tf_op jit(solution)/shard_map/third/pallas_call | solution.py:563
where the time goes:
time: 174 us
  Pallas kernels  174 us (100%)
    pallas_call x1, Pallas kernels, body(): pl.pallas_call(functools.partial(second_kernel, total), in_specs=[outside...  84.9 us
    pallas_call x1, Pallas kernels, body(): pl.pallas_call(functools.partial(first_kernel, total), in_specs=[outside]...  75.7 us
    pallas_call x1, Pallas kernels, body(): pl.pallas_call(functools.partial(third_kernel, total), grid=(local // (2...  13.1 us

commit v1 on v0

--- a/solution.py
+++ b/solution.py
@@ -311,9 +311,10 @@
     for j in range(3):
         gram_columns(j)
     advance(rest)
-    for _ in range(7):
+    for _ in range(6):
         advance(lead)
         advance(rest)
+    advance(lead)
 
     for n in range(4):
         value = (sums[span(n, WIDTH), :] * scale).astype(BF16)
@@ -322,11 +323,19 @@
 
     @pl.loop(0, earlier.shape[0] // (2 * STEP))
     def _(n):
-        for k in range(2):
-            at = pl.ds(pl.multiple_of((2 * n + k) * STEP, STEP), STEP)
-            flat = panels[at, :].astype(F32) - dot(earlier[at, :], coeffs[:WIDTH, :])
-            top_all[at, :] = flat[:, :PANEL].astype(BF16)
-            flat_all[at, :] = flat[:, PANEL:]
+        at = pl.ds(pl.multiple_of(n * STEP, STEP), STEP)
+        flat = panels[at, :].astype(F32) - dot(earlier[at, :], coeffs[:WIDTH, :])
+        top_all[at, :] = flat[:, :PANEL].astype(BF16)
+        flat_all[at, :] = flat[:, PANEL:]
+
+    advance(rest)
+
+    @pl.loop(earlier.shape[0] // (2 * STEP), earlier.shape[0] // STEP)
+    def _(n):
+        at = pl.ds(pl.multiple_of(n * STEP, STEP), STEP)
+        flat = panels[at, :].astype(F32) - dot(earlier[at, :], coeffs[:WIDTH, :])
+        top_all[at, :] = flat[:, :PANEL].astype(BF16)
+        flat_all[at, :] = flat[:, PANEL:]
 
     saves = [pltpu.make_async_copy(flat_all, flat_hbm, save.at[0])]
     saves[0].start()

time: 174 us -> 172 us (0.989)
  Pallas kernels: 174 us -> 171 us
    pallas_call x1, Pallas kernels: 84.9 us -> 82.4 us  [body(): pl.pallas_call(functools.partial(second_kernel, total), in_specs=[outside...]
where the time goes in v1:
time: 172 us
  Pallas kernels  171 us (99%)
    pallas_call x1, Pallas kernels, body(): pl.pallas_call(functools.partial(second_kernel, total), in_specs=[outside...  82.4 us
    pallas_call x1, Pallas kernels, body(): pl.pallas_call(functools.partial(first_kernel, total), in_specs=[outside]...  75.7 us
    pallas_call x1, Pallas kernels, body(): pl.pallas_call(functools.partial(third_kernel, total), grid=(local // (2...  13.1 us

profile of v1, /device:TPU:1, one launch (start us, length us, event | category | flops | bytes accessed | tf_op | source)
XLA Modules:
  0.0 171.9 jit_solution(6971424240452147161)
XLA Ops:
  0.6 75.7 %first.1 = (bf16[4096,256]{1,0:T(8,128)(2,1)}, bf16[4096,256]{1,0:T(8,128)(2,1)}, f32[4096,256]{1,0:T(8,128)}, f32[1024,256]{1,0:T(8,128)}, f32[1024,256]{1,0:T(...) custom-call(bf16[4096,1024]{1,0:T(8,128)(2,1)} %earlier_hbm.3, bf16[4096,512]{1,0:T(8,128)(2,1)} %panels_hbm.1), custom_call_target="tpu_custom_call" | custom-call | tf_op jit(solution)/shard_map/first/pallas_call | solution.py:539
  76.3 82.4 %second.1 = (bf16[4096,256]{1,0:T(8,128)(2,1)}, f32[256,256]{1,0:T(8,128)}, bf16[4096,256]{1,0:T(8,128)(2,1)}, bf16[4096,256]{1,0:T(8,128)(2,1)}, f32[3072,128]{1,0:T(8,128)}) custom-call(f32[1024,128]{1,0:T(8,128)} %get-tuple-element.18.part_hbm, f32[1024,256]{1,0:T(8,128)} %get-tuple-element.19.left_hbm, f32[1024,256]{1,0:T(8,128)} %get-tuple-element.20.second_hbm, ...), custom_call_target="tpu_custom_call" | custom-call | tf_op jit(solution)/shard_map/second/pallas_call | solution.py:557
  158.8 13.1 %third.1 = (f32[2,256,256]{2,1,0:T(8,128)}, f32[512,512]{1,0:T(8,128)}, bf16[4096,512]{1,0:T(8,128)(2,1)}) custom-call(f32[3072,128]{1,0:T(8,128)} %get-tuple-element.25.sums_ref, f32[256,256]{1,0:T(8,128)} %get-tuple-element.26.first_upper_ref, bf16[4096,256]{1,0:T(8,128)(2,1)} %get-tuple-element.27.first_ref, bf16[4096,256]{1,0:T(8,128)(2,1)} %get-tuple-element.28.top_ref, ...), custom_call_target="tpu_custom_call" | custom-call | tf_op jit(solution)/shard_map/third/pallas_call | solution.py:572
